TPU v7x, 256 devices: a whole 4x4x8 slice. The times are simulated.
256 devices in a mesh: fsdp: 16 (over z, y_hi), cols: 16 (over y_lo, x, core).
Axes of the slice: x: 4, y: 4 (y_hi: 2, y_lo: 2; y = y_hi * 2 + y_lo), z: 8, core: 2. Of those that a mesh axis runs over, the one named last changes fastest.
Arguments:
- train_gate: bfloat16 [3584, 14336], P('fsdp', 'cols'), may hold values from -0.09375 to 0.09375
- low_gate: bfloat16 [3584, 16], P('fsdp'), may hold values from -0.09375 to 0.09375
- high_gate: bfloat16 [16, 14336], P(None, 'cols'), may hold values from -1.5 to 1.5
- train_up: bfloat16 [3584, 14336], P('fsdp', 'cols'), may hold values from -0.09375 to 0.09375
- low_up: bfloat16 [3584, 16], P('fsdp'), may hold values from -0.09375 to 0.09375
- high_up: bfloat16 [16, 14336], P(None, 'cols'), may hold values from -1.5 to 1.5
- train_down: bfloat16 [14336, 3584], P('cols', 'fsdp'), may hold values from -0.046875 to 0.046875
- low_down: bfloat16 [14336, 16], P('cols'), may hold values from -0.046875 to 0.046875
- high_down: bfloat16 [16, 3584], P(None, 'fsdp'), may hold values from -1.5 to 1.5
- norm_train: float32 [3584], P(('fsdp', 'cols')), may hold values from 0.25 to 1.75
- norm_step: float32 [3584], P(('fsdp', 'cols')), may hold values from -0.3 to 0.3
Outputs:
- serving_gate: bfloat16 [3584, 14336], P(None, 'cols')
- serving_up: bfloat16 [3584, 14336], P(None, 'cols')
- serving_down: bfloat16 [14336, 3584], P('cols')
- serve_norm: bfloat16 [3584], replicated
All inputs are finite; a program needn't handle non-finite values.
Results may differ from a plain program's by a relative error of at most 0.001.
Values may be sent and summed in bfloat16 or wider, within the bound.
No kernel may reach another device: no remote copies, remote signals or barrier semaphores. Data moves between devices by JAX's collectives and lax.ppermute only.
A program may use at most 128 MiB of HBM per device.

v0:
```python
import jax
import jax.numpy as jnp
from jax import lax
from jax.sharding import PartitionSpec as P

mix_rate = 1.0


def rows_first(arrays, axis, dims):
    turned = [jnp.moveaxis(a, dim, 0) for a, dim in zip(arrays, dims)]
    both = jnp.concatenate([t.reshape(len(t), -1) for t in turned], axis=1)
    out, at, outs = (lax.all_gather(both, axis, axis=0, tiled=True), 0, [])
    for t, dim in zip(turned, dims):
        slab = out[:, at : at + t[0].size].reshape(-1, *t.shape[1:])
        outs.append(jnp.moveaxis(slab, 0, dim))
        at += t[0].size
    return tuple(outs)


def per_device(
    train_gate,
    low_gate,
    high_gate,
    train_up,
    low_up,
    high_up,
    train_down,
    low_down,
    high_down,
    norm_train,
    norm_step,
):
    whole_gate = train_gate.astype(jnp.float32) + mix_rate * jnp.dot(
        low_gate, high_gate, preferred_element_type=jnp.float32
    )
    whole_up = train_up.astype(jnp.float32) + mix_rate * jnp.dot(
        low_up, high_up, preferred_element_type=jnp.float32
    )
    whole_down = train_down.astype(jnp.float32) + mix_rate * jnp.dot(
        low_down, high_down, preferred_element_type=jnp.float32
    )
    narrow_gate, narrow_up, narrow_down = (
        whole_gate.astype(jnp.bfloat16),
        whole_up.astype(jnp.bfloat16),
        whole_down.astype(jnp.bfloat16),
    )
    serving_gate, serving_up, serving_down = rows_first(
        (narrow_gate, narrow_up, narrow_down), "fsdp", (0, 0, 1)
    )
    serve_norm = lax.all_gather(
        (norm_train + norm_step).astype(jnp.bfloat16), ("fsdp", "cols"), axis=0, tiled=True
    )
    return (serving_gate, serving_up, serving_down, serve_norm)


def solution(mesh):
    return jax.shard_map(
        per_device,
        mesh=mesh,
        in_specs=(
            P("fsdp", "cols"),
            P("fsdp", None),
            P(None, "cols"),
            P("fsdp", "cols"),
            P("fsdp", None),
            P(None, "cols"),
            P("cols", "fsdp"),
            P("cols", None),
            P(None, "fsdp"),
            P(("fsdp", "cols")),
            P(("fsdp", "cols")),
        ),
        out_specs=(P(None, "cols"), P(None, "cols"), P("cols", None), P()),
        check_vma=False,
    )
```

profile of v0, /device:TPU:1, one launch (start us, length us, event | category | flops | bytes accessed | tf_op | source)
XLA Modules:
  0.0 301.7 jit_solution(67208381330792148)
XLA Ops:
  7.2 0.0 copy-start
  7.2 0.0 all-gather.2.cloned.1.call-start
  7.2 0.7 copy-done
  7.9 1.3 fusion
  9.2 1.3 fusion.1
  10.6 0.0 copy-start.1
  10.6 0.0 copy-start.2
  10.6 1.4 fusion.3
  12.0 1.1 pad_maximum_fusion
  13.1 0.0 all-gather.2.cloned.1.call-update
  13.1 0.0 copy-done.1
  13.1 0.0 copy-done.2
  13.1 0.2 dynamic-update-slice
  13.4 189.9 %all-reduce = bf16[3584]{0:T(1024)(128)(2,1)} all-reduce(bf16[3584]{0:T(1024)(128)(2,1)S(1)} %dynamic-update-slice), channel_id=1, replica_groups=mesh['fsdp'=16,'cols'=16] {'fsdp','cols'}, use_global_device_ids=true, to_apply=%add | all-reduce | flops 3584 | bytes 14336
  203.3 67.5 %all-gather.2.cloned.1.call-done = bf16[3584,2688]{1,0:T(8,128)(2,1)} async-done(((bf16[224,2688]{1,0:T(8,128)(2,1)}), bf16[3584,2688]{1,0:T(8,128)(2,1)}) %all-gather.2.cloned.1.call-update) | async-done | bytes 19267600 | tf_op jit(solution)/shard_map/all_gather | solution.py:12
  270.8 14.6 %slice_bitcast_fusion = (bf16[896,3584]{0,1:T(8,128)(2,1)}, bf16[3584,896]{1,0:T(8,128)(2,1)}, bf16[3584,896]{1,0:T(8,128)(2,1)}) fusion(bf16[3584,2688]{1,0:T(8,128)(2,1)} %all-gather.2.cloned.1.call-done), kind=kLoop, calls=%fused_computation | loop fusion | bytes 38535168 | tf_op jit(solution)/shard_map/transpose | solution.py:15
  285.4 9.5 %copy.15 = bf16[896,3584]{1,0:T(8,128)(2,1)} copy(bf16[896,3584]{0,1:T(8,128)(2,1)} %get-tuple-element.8) | data formatting | bytes 12845056
  (2 shorter events, 0.0 us)
Async XLA Ops:
  7.2 0.8 copy-start
  7.2 263.6 %all-gather.2.cloned.1.call-start = ((), (), s32[]{:S(2)}) async-start(), calls=%async_computation | async-start | bytes 20471808 | tf_op jit(solution)/shard_map/all_gather | solution.py:12
  10.6 2.5 copy-start.1
  10.6 2.5 copy-start.2
Sparse Core Ops, SparseCore 0:
  13.2 257.5 all-gather.1
where the time goes:
time: 302 us
  blocking collectives  190 us (63%)
  waiting for transfers between devices  67.5 us (22%)
  local copies, waits for them, and re-layouts  25.1 us (8%)
  between operations  14.1 us (5%)
  matrix products  4 us (1%)
    unnamed x1, blocking collectives  190 us
    all_gather x1, waiting for transfers between devices, rows_first(): out, at, outs = (lax.all_gather(both, axis, axis=0, tiled=True), 0, [])  67.5 us
    transpose x1, local copies, waits for them, and re-layouts, rows_first(): outs.append(jnp.moveaxis(slab, 0, dim))  14.6 us
    unnamed x9, local copies, waits for them, and re-layouts  10.5 us
  transfers between devices with their start and end apart: 1, of which 1 were waited for; matrix products, arithmetic and copies ran while one was open for 0% of the time, Pallas kernels for 0%

commit v1 on v0

--- a/solution.py
+++ b/solution.py
@@ -6,10 +6,15 @@
 mix_rate = 1.0
 
 
+def gather_over(value, axis, along):
+    sent = jnp.stack([value] * lax.axis_size(axis))
+    return jnp.concatenate(lax.all_to_all(sent, axis, 0, 0), axis=along)
+
+
 def rows_first(arrays, axis, dims):
     turned = [jnp.moveaxis(a, dim, 0) for a, dim in zip(arrays, dims)]
     both = jnp.concatenate([t.reshape(len(t), -1) for t in turned], axis=1)
-    out, at, outs = (lax.all_gather(both, axis, axis=0, tiled=True), 0, [])
+    out, at, outs = (gather_over(both, axis, 0), 0, [])
     for t, dim in zip(turned, dims):
         slab = out[:, at : at + t[0].size].reshape(-1, *t.shape[1:])
         outs.append(jnp.moveaxis(slab, 0, dim))

time: 302 us -> 534 us (1.77)
  blocking collectives: 190 us -> 485 us
  waiting for transfers between devices: 67.5 us -> 0.01 us
  between operations: 14.1 us -> 0.72 us
  starting transfers between devices: 0.04 us -> 11.9 us
  local copies, waits for them, and re-layouts: 25.1 us -> 31.8 us
    unnamed x1, blocking collectives: 190 us -> 485 us
    all_gather x1 -> x0, waiting for transfers between devices: 67.5 us -> none  [rows_first(): out, at, outs = (lax.all_gather(both, axis, axis=0, tiled=True), 0, [])]
    all_to_all x0 -> x1, starting transfers between devices: none -> 11.9 us  [gather_over(): return jnp.concatenate(lax.all_to_all(sent, axis, 0, 0), axis=along)]
    another operation x0 -> x1, local copies, waits for them, and re-layouts: none -> 6.71 us  [gather_over(): sent = jnp.stack([value] * lax.axis_size(axis))]
  transfers between devices with their start and end apart: 1 -> 1, of which waited for: 1 -> 0; matrix products, arithmetic and copies ran while one was open for 0% -> 0% of each run, Pallas kernels for 0% -> 0%
where the time goes in v1:
time: 534 us; the launch traced here: 533 us
  blocking collectives  485 us (91%)
  local copies, waits for them, and re-layouts  31.8 us (6%)
  starting transfers between devices  11.9 us (2%)
    unnamed x1, blocking collectives  485 us
    transpose x1, local copies, waits for them, and re-layouts, rows_first(): outs.append(jnp.moveaxis(slab, 0, dim))  14.6 us
    all_to_all x1, starting transfers between devices, gather_over(): return jnp.concatenate(lax.all_to_all(sent, axis, 0, 0), axis=along)  11.9 us
  transfers between devices with their start and end apart: 1, of which 0 were waited for; matrix products, arithmetic and copies ran while one was open for 0% of the time, Pallas kernels for 0%

profile of v1, /device:TPU:1, one launch (start us, length us, event | category | flops | bytes accessed | tf_op | source)
XLA Modules:
  0.0 533.4 jit_solution(11799049675258787030)
XLA Ops:
  0.6 0.0 copy-start
  0.6 0.7 copy-done
  1.4 1.3 fusion
  2.7 1.3 fusion.1
  4.0 1.3 fusion.3
  5.4 0.1 pad_maximum_fusion
  5.5 6.7 %stack.2 = bf16[16,224,2688]{2,1,0:T(8,128)(2,1)} broadcast(bf16[224,2688]{1,0:T(8,128)(2,1)S(1)} %pad_maximum_fusion), dimensions={1,2} | broadcast | bytes 20471808 | tf_op jit(solution)/shard_map/stack | solution.py:10
  12.2 0.0 copy-start.2
  12.2 0.0 copy-start.3
  12.2 11.9 %all-to-all-start = ((bf16[16,224,2688]{2,1,0:T(8,128)(2,1)}), bf16[16,224,2688]{2,1,0:T(8,128)(2,1)}, u32[]{:S(2)}, u32[]{:S(2)}) async-start(bf16[16,224,2688]{2,1,0:T(8,128)(2,1)} %stack.2), calls=%async_computation | async-start | bytes 38535168 | tf_op jit(solution)/shard_map/all_to_all | solution.py:11
  24.1 0.0 copy-done.2
  24.2 0.0 copy-done.3
  24.2 0.2 dynamic-update-slice
  24.4 484.9 %all-reduce = bf16[3584]{0:T(1024)(128)(2,1)} all-reduce(bf16[3584]{0:T(1024)(128)(2,1)S(1)} %dynamic-update-slice), channel_id=1, replica_groups=mesh['fsdp'=16,'cols'=16] {'fsdp','cols'}, use_global_device_ids=true, to_apply=%add | all-reduce | flops 3584 | bytes 14336
  509.3 0.0 all-to-all-done
  509.3 14.6 %slice_bitcast_fusion = (bf16[896,3584]{0,1:T(8,128)(2,1)}, bf16[3584,896]{1,0:T(8,128)(2,1)}, bf16[3584,896]{1,0:T(8,128)(2,1)}) fusion(bf16[3584,2688]{1,0:T(8,128)(2,1)} %bitcast.1), kind=kLoop, calls=%fused_computation | loop fusion | bytes 38535168 | tf_op jit(solution)/shard_map/transpose | solution.py:20
  523.9 0.0 copy-start.1
  523.9 9.5 %copy.18 = bf16[896,3584]{1,0:T(8,128)(2,1)} copy(bf16[896,3584]{0,1:T(8,128)(2,1)} %get-tuple-element.12) | data formatting | bytes 12845056
  533.4 0.0 copy-done.1
  (2 shorter events, 0.0 us)
Async XLA Ops:
  0.6 0.8 copy-start
  12.2 11.9 %copy-start.2 = (f32[14]{0:T(128)S(1)}, f32[14]{0:T(128)}, u32[]{:S(2)}) copy-start(f32[14]{0:T(128)} %param.20) | copy-start | bytes 172
  12.2 11.9 %copy-start.3 = (f32[14]{0:T(128)S(1)}, f32[14]{0:T(128)}, u32[]{:S(2)}) copy-start(f32[14]{0:T(128)} %param.21) | copy-start | bytes 172
  12.2 497.1 %all-to-all-start = ((bf16[16,224,2688]{2,1,0:T(8,128)(2,1)}), bf16[16,224,2688]{2,1,0:T(8,128)(2,1)}, u32[]{:S(2)}, u32[]{:S(2)}) async-start(bf16[16,224,2688]{2,1,0:T(8,128)(2,1)} %stack.2), calls=%async_computation | async-start | bytes 38535168 | tf_op jit(solution)/shard_map/all_to_all | solution.py:11
  523.9 9.5 %copy-start.1 = (bf16[16,896]{1,0:T(8,128)(2,1)S(1)}, bf16[16,896]{1,0:T(8,128)(2,1)}, u32[]{:S(2)}) copy-start(bf16[16,896]{1,0:T(8,128)(2,1)} %param.13) | copy-start | bytes 86020
